TPU v7x, 32 devices: a whole 2x2x4 slice. The times are simulated.
32 devices in a mesh: field: 2 (over core), dom: 16 (over z, y, x).
Axes of the slice: x: 2, y: 2, z: 4, core: 2. Of those that a mesh axis runs over, the one named last changes fastest.
Arguments:
- modes: float32 [2, 40, 131072], P('field', None, 'dom'), may hold values from -6 to 6
- previous: float32 [2, 40, 131072], P('field', None, 'dom'), may hold values from -6 to 6
- kinds: int32 [2, 3, 256], P('field'), may hold values from 0 to 3
- scales: float32 [2, 3, 256], P('field'), may hold values from 0.5 to 4
- tables: bfloat16 [2, 3, 4, 512, 512], P('field'), may hold values from -2 to 6, as said below
- wet_rows: int32 [2, 49152], P('field', 'dom'), may hold values from 0 to 8191, as said below
- wet_counts: int32 [16], P('dom'), may hold values from 768 to 3072, as said below
- coupling: float32 [49152], P('dom'), may hold values from -6 to 6
Outputs:
- basis: float32 [2, 120, 131072], P('field', None, 'dom')
- projected: float32 [120, 120], replicated
Inputs may be any that keep to these rules, and one draw needn't show every extreme that they name: `tables`: tables of offset 0 are symmetric. `wet_rows`: within each subdomain and field the 3072 row numbers are distinct. `wet_counts`: some subdomain uses all 3072 slots.
All inputs are finite; a program needn't handle non-finite values.
Results may differ from a plain program's by a relative error of at most 0.00045.
The roundings to bfloat16 on the way count: a program that leaves them out, or rounds other values in their place, can miss the bound.
Values may be sent and summed in bfloat16 or wider, within the bound.
A program may use at most 192 MiB of HBM per device.

v0:
```python
import jax
import jax.numpy as jnp
from jax import lax
from jax.sharding import PartitionSpec as P

BS = 512
NTYPE = 4
NBR = 16
IFACE = 3072


def for_sending(shard):
    return jax.tree.map(lambda a: a.astype(jnp.bfloat16) if a.dtype == jnp.float32 else a, shard)


def swapped(shard, axis, apart):
    return lax.ppermute(shard, axis, [(i, i ^ 1 << apart) for i in range(lax.axis_size(axis))])


def extended(cells, sides, width):
    for axis, dim in sides:
        count = lax.axis_size(axis)
        ends = count - 1
        head = lax.slice_in_dim(cells, 0, width, axis=dim)
        tail = lax.slice_in_dim(cells, cells.shape[dim] - width, cells.shape[dim], axis=dim)
        cells = jnp.concatenate(
            [
                lax.ppermute(tail, axis, [(i, (i + 1) % count) for i in range(ends)]),
                cells,
                lax.ppermute(head, axis, [((i + 1) % count, i) for i in range(ends)]),
            ],
            axis=dim,
        )
    return cells


def typed_product(blocks, table_set, type_ids, factors, transposed):
    columns = blocks.shape[0]
    count = blocks.shape[1]
    flattened = blocks.reshape(columns * count, BS)
    contract = 0 if transposed else 1
    result = jnp.zeros((columns, count, BS), jnp.float32)
    for type_id in range(NTYPE):
        product = lax.dot_general(
            flattened,
            table_set[type_id],
            (((1,), (contract,)), ((), ())),
            preferred_element_type=jnp.float32,
        )
        factor_t = jnp.where(type_ids == type_id, factors, jnp.float32(0.0))
        result = result + factor_t[None, :, None] * product.reshape(columns, count, BS)
    return result


def block_product(window, kinds, scales, tables):
    columns = window.shape[0]
    blocks = window.reshape(columns, NBR + 4, BS)
    result = typed_product(blocks[:, 2 : NBR + 2], tables[0], kinds[0, 2:], scales[0, 2:], False)
    for offset in (1, 2):
        result = result + typed_product(
            blocks[:, 2 + offset : NBR + 2 + offset],
            tables[offset],
            kinds[offset, 2:],
            scales[offset, 2:],
            False,
        )
        result = result + typed_product(
            blocks[:, 2 - offset : NBR + 2 - offset],
            tables[offset],
            kinds[offset, 2 - offset : NBR + 2 - offset],
            scales[offset, 2 - offset : NBR + 2 - offset],
            True,
        )
    return result.reshape(columns, NBR * BS)


def operate(window, vectors, kinds, scales, tables, rows, weights):
    images = block_product(window, kinds, scales, tables)
    values = jnp.take(vectors, rows, axis=1) * weights[None, :]
    received = swapped(for_sending(values), "field", 0).astype(values.dtype)
    return images.at[:, rows].add(received)


def shards(modes, previous, kinds, scales, tables, wet_rows, wet_counts, coupling):
    highest = lax.Precision.HIGHEST
    domain = lax.axis_index("dom")
    vec_modes = modes[0]
    vec_prev = previous[0]
    field_tables = tables[0]
    kinds_pad = jnp.pad(kinds[0], ((0, 0), (2, 0)))
    scales_pad = jnp.pad(scales[0], ((0, 0), (2, 0)))
    local_kinds = lax.dynamic_slice_in_dim(kinds_pad, domain * NBR, NBR + 2, 1)
    local_scales = lax.dynamic_slice_in_dim(scales_pad, domain * NBR, NBR + 2, 1)
    rows = wet_rows[0]
    used = jnp.arange(IFACE, dtype=jnp.int32) < wet_counts[0]
    weights = jnp.where(used, coupling, jnp.float32(0.0))
    window_modes = extended(vec_modes.astype(jnp.bfloat16), (("dom", 1),), 2 * BS)
    image_x = operate(
        window_modes, vec_modes, local_kinds, local_scales, field_tables, rows, weights
    )
    squares, products = lax.psum(
        (jnp.sum(vec_modes * vec_modes, axis=1), jnp.sum(vec_modes * image_x, axis=1)),
        ("field", "dom"),
    )
    quotient = products / squares
    diag_table = jnp.diagonal(field_tables[0], axis1=1, axis2=2).astype(jnp.float32)
    selector = (local_kinds[0, 2:][:, None] == jnp.arange(NTYPE, dtype=jnp.int32)[None, :]).astype(
        jnp.float32
    )
    row_diag = jnp.dot(selector, diag_table, precision=highest)
    jacobi = (local_scales[0, 2:][:, None] * row_diag).reshape(NBR * BS)
    residual_dir = (image_x - vec_modes * quotient[:, None]) / jacobi[None, :]
    pair = jnp.concatenate([residual_dir, vec_prev], axis=0)
    window_pair = extended(pair.astype(jnp.bfloat16), (("dom", 1),), 2 * BS)
    image_wp = operate(window_pair, pair, local_kinds, local_scales, field_tables, rows, weights)
    search = jnp.concatenate([vec_modes, pair], axis=0)
    image_all = jnp.concatenate([image_x, image_wp], axis=0)
    ndof = 2.0 * lax.axis_size("dom") * NBR * BS
    summed_b, summed_a = lax.psum(
        (
            jnp.dot(search, search.T, precision=highest),
            jnp.dot(search, image_all.T, precision=highest),
        ),
        ("field", "dom"),
    )
    gram_b = summed_b / ndof
    gram_a = (summed_a + summed_a.T) / (2.0 * ndof)
    chol = jnp.linalg.cholesky(gram_b)
    leading = jax.scipy.linalg.solve_triangular(chol, gram_a, lower=True)
    projected = jax.scipy.linalg.solve_triangular(chol, leading.T, lower=True)
    basis = jax.scipy.linalg.solve_triangular(chol, search, lower=True)
    return (basis[None], projected)


def solution(mesh):
    return jax.shard_map(
        shards,
        mesh=mesh,
        in_specs=(
            P("field", None, "dom"),
            P("field", None, "dom"),
            P("field", None, None),
            P("field", None, None),
            P("field", None, None, None, None),
            P("field", "dom"),
            P("dom"),
            P("dom"),
        ),
        out_specs=(P("field", None, "dom"), P()),
        check_vma=False,
    )
```

profile of v0, /device:TPU:0, one launch (start us, length us, event | category | flops | bytes accessed | tf_op | source)
XLA Modules:
  0.0 542.5 jit_solution(1693732785863256557)
XLA Ops:
  7.2 3.7 copy.30
  10.9 2.4 bitcast_convert_fusion
  14.2 5.6 %collective-permute-start = (bf16[40,1024]{0,1:T(8,128)(2,1)}, bf16[40,1024]{0,1:T(8,128)(2,1)}, u32[]{:S(2)}, u32[]{:S(2)}) collective-permute-start(bf16[40,1024]{0,1:T(8,128)(2,1)} %get-tuple-element.18), channel_id=1, source_target_pairs={{0,1},{1,2},{2,3},{3,4},{4,5},{5,6},{6,7},{7,8},{8,9},{9,10},{10,1... | collective-permute-start | bytes 245768 | tf_op jit(solution)/shard_map/ppermute | solution.py:28
  19.7 1.3 collective-permute-start.1
  21.7 13.1 %gather_fusion = f32[3072,40]{1,0:T(8,128)} fusion(f32[40,8192]{0,1:T(8,128)} %bitcast.254, s32[3072]{0:T(1024)S(1)} %broadcast_clamp_fusion), kind=kCustom, calls=%fused_computation | custom fusion | bytes 995328 | tf_op jit(solution)/shard_map/jit(_take)/gather | solution.py:79
  34.9 2.8 fusion.24
  38.6 1.5 copy.32
  40.6 1.1 slice-done.8
  41.7 41.6 %copy.52 = bf16[1,1,4,512,512]{2,4,3,1,0:T(8,128)(2,1)} copy(bf16[1,1,4,512,512]{4,3,2,1,0:T(8,128)(2,1)S(1)} %slice-done.8) | data formatting | bytes 4194304
  83.3 6.5 %gather_fusion.1 = bf16[512,4]{1,0:T(8,128)(2,1)S(1)} fusion(bf16[4,512,512]{0,2,1:T(8,128)(2,1)} %bitcast.58, s32[512]{0:T(512)S(1)} %bitcast.269), kind=kCustom, calls=%fused_computation.1 | custom fusion | bytes 12288 | tf_op jit(solution)/shard_map/jit(diagonal)/gather | solution.py:106
  90.0 3.9 copy.38
  95.7 1.7 convolution_multiply_fusion.19
  97.4 1.6 convolution_multiply_fusion.15
  99.0 1.7 convolution_multiply_fusion.11
  100.8 1.6 convolution_multiply_fusion.7
  102.3 1.5 convolution_multiply_fusion.3
  112.1 2.7 copy.47
  116.3 19.6 %scatter_fusion = f32[40,8192]{0,1:T(8,128)} fusion(f32[40,8192]{0,1:T(8,128)} %bitcast.256, s32[3072]{0:T(1024)S(1)} %bitcast.271, f32[3072,40]{1,0:T(8,128)S(1)} %copy.36), kind=kCustom, calls=%fused_computation.3 | custom fusion | flops 122880 | bytes 1486848 | tf_op jit(solution)/shard_map/scatter-add | solution.py:81
  135.9 4.6 multiply_reduce_fusion
  140.4 41.7 %all-reduce.3 = (f32[40]{0:T(128)S(1)}, f32[40]{0:T(128)S(1)}) all-reduce(f32[40]{0:T(128)S(1)} %get-tuple-element.4, f32[40]{0:T(128)S(1)} %get-tuple-element.3), channel_id=1, replica_groups=mesh['field'=2,'dom'=16] {'field','dom'}, use_global_device_ids=true, to_apply=%region_2.3 | all-reduce | flops 80 | bytes 640 | tf_op jit(solution)/shard_map/psum | solution.py:101
  182.2 6.0 %subtract_divide_fusion = f32[40,8192]{0,1:T(8,128)S(1)} fusion(f32[40,8192]{0,1:T(8,128)} %scatter_fusion, f32[8192]{0:T(1024)S(1)} %bitcast.273, f32[40]{0:T(128)S(1)} %div.33, f32[1,40,8192]{1,2,0:T(8,128)} %copy.30), kind=kLoop, calls=%fused_computation.12 | loop fusion | flops 983040 | bytes 3965088 | tf_op jit(solution)/shard_map/div | solution.py:112
  188.2 3.2 fusion.174
  191.3 4.2 pad_maximum_fusion
  196.4 4.2 collective-permute-start.3
  200.6 1.3 collective-permute-start.4
  201.9 13.5 %gather_fusion.2 = f32[3072,80]{1,0:T(8,128)} fusion(f32[80,8192]{0,1:T(8,128)} %get-tuple-element.10, s32[3072]{0:T(1024)S(1)} %broadcast_clamp_fusion), kind=kCustom, calls=%fused_computation.2 | custom fusion | bytes 1978368 | tf_op jit(solution)/shard_map/jit(_take)/gather | solution.py:79
  215.4 2.8 fusion.25
  219.3 10.8 %fusion.178 = f32[120,120]{0,1:T(8,128)} fusion(f32[120,8192]{0,1:T(8,128)} %pad_maximum_fusion), kind=kOutput, calls=%fused_computation.259 | convolution fusion | flops 1415577600 | bytes 3989760 | tf_op jit(solution)/shard_map/dot_general | solution.py:121
  230.1 7.7 %pad_maximum_fusion.2 = bf16[80,10240]{0,1:T(8,128)(2,1)S(1)} fusion(bf16[80,1024]{0,1:T(8,128)(2,1)S(1)} %collective-permute-done.4, bf16[80,8192]{0,1:T(8,128)(2,1)S(1)} %get-tuple-element.9, bf16[80,1024]{0,1:T(8,128)(2,1)S(1)} %collective-permute-done.3), kind=kLoop, calls=%fused_computation.15 | loop fusion | flops 4915200 | bytes 3276800 | tf_op jit(solution)/shard_map/concatenate | solution.py:26
  237.8 4.2 fusion.175
  242.0 3.2 copy.53
  245.3 3.6 fusion.26
  248.8 3.4 fusion.29
  252.2 2.4 fusion.32
  254.6 2.3 fusion.35
  256.9 3.1 copy.56
  260.0 3.8 fusion.39
  263.8 3.6 fusion.45
  267.4 3.1 copy.57
  270.5 3.5 fusion.43
  274.0 3.5 fusion.49
  277.5 2.4 fusion.51
  279.9 2.4 fusion.55
  282.3 2.3 fusion.57
  284.6 3.1 copy.55
  287.7 1.1 copy-done.2
  288.8 3.4 fusion.61
  292.1 3.9 fusion.67
  296.0 4.4 copy.54
  300.5 4.0 fusion.63
  304.5 4.0 fusion.69
  308.5 2.3 fusion.73
  310.8 2.4 fusion.75
  313.2 2.3 fusion.79
  315.5 2.4 fusion.81
  317.9 19.0 %add_add_fusion = f32[80,16,512]{2,1,0:T(8,128)} fusion(f32[80,16,512]{2,1,0:T(8,128)} %fusion.43, f32[80,16,512]{2,1,0:T(8,128)} %fusion.49, f32[80,16,512]{2,1,0:T(8,128)} %fusion.55, f32[80,16,512]{2,1,0:T(8,128)} %fusion.39, f32[80,16,512]{2,1,0:T(8,128)} %fusion.45, f32[80,16,512]{2,1,0:T(8,128)} %fusion.51, f32[80,16,512]{2,1,0:T(8,128)} %fusion.57, ...), kind=kOutput, calls=%fused_computation.16 | convolution fusion | flops 696647680 | bytes 54265088 | tf_op jit(solution)/shard_map/dot_general | solution.py:44
  336.9 4.9 copy.49
  341.8 1.1 convert_bitcast_fusion
  343.4 19.6 %scatter_fusion.1 = f32[80,8192]{0,1:T(8,128)} fusion(f32[80,8192]{0,1:T(8,128)} %bitcast.258, s32[3072]{0:T(1024)S(1)} %bitcast.272, f32[3072,80]{1,0:T(8,128)S(1)} %copy.44), kind=kCustom, calls=%fused_computation.4 | custom fusion | flops 245760 | bytes 2961408 | tf_op jit(solution)/shard_map/scatter-add | solution.py:81
  363.0 13.1 %fusion = f32[120,120]{1,0:T(8,128)} fusion(f32[120,8192]{0,1:T(8,128)} %pad_maximum_fusion, f32[80,8192]{0,1:T(8,128)} %scatter_fusion.1, f32[40,8192]{0,1:T(8,128)} %scatter_fusion), kind=kOutput, calls=%fused_computation.8 | convolution fusion | flops 1416560640 | bytes 7921920 | tf_op jit(solution)/shard_map/dot_general | solution.py:122
  376.2 125.3 %all-reduce.6.cloned.1.call-done = (f32[120,120]{0,1:T(8,128)}, f32[120,120]{1,0:T(8,128)}) async-done(((f32[120,120]{0,1:T(8,128)}, f32[120,120]{1,0:T(8,128)}), (f32[120,120]{0,1:T(8,128)}, f32[120,120]{1,0:T(8,128)})) %all-reduce.6.cloned.1.call-update) | async-done | bytes 115216 | tf_op jit(solution)/shard_map/psum | solution.py:119
  503.3 11.0 %cholesky.16 = f32[120,120]{1,0:T(8,128)S(1)} custom-call(f32[120,120]{1,0:T(8,128)S(1)} %fusion.152), custom_call_target="Cholesky" | custom-call | tf_op jit(solution)/shard_map/jit(cholesky)/cholesky | solution.py:128
  515.6 9.5 %custom-call.10 = f32[1,120,120]{1,2,0:T(8,128)S(1)} custom-call(f32[1,120,120]{2,1,0:T(8,128)S(1)} %fusion.145), custom_call_target="InvertDiagBlocksLowerTriangular" | custom-call | tf_op jit(solution)/shard_map/jit(_solve_triangular)/triangular_solve | solution.py:131
  526.0 7.9 %convolution_bitcast_fusion = f32[1,120,8192]{2,1,0:T(8,128)} fusion(f32[120,8192]{0,1:T(8,128)} %pad_maximum_fusion, f32[1,120,120]{1,2,0:T(8,128)S(1)} %custom-call.10), kind=kOutput, calls=%fused_computation.5 | convolution fusion | flops 1415577600 | bytes 7921920 | tf_op jit(solution)/shard_map/jit(_solve_triangular)/triangular_solve | solution.py:131
  (107 shorter events, 21.6 us)
Async XLA Ops:
  7.2 494.4 %all-reduce.6.cloned.1.call-start = ((), (), s32[]{:S(2)}) async-start(), calls=%async_computation | async-start | bytes 245760 | tf_op jit(solution)/shard_map/psum | solution.py:119
  10.9 10.1 %copy-start.9 = (s32[1,3072]{1,0:T(1,128)S(1)}, s32[1,3072]{1,0:T(1,128)}, u32[]{:S(2)}) copy-start(s32[1,3072]{1,0:T(1,128)} %param.15) | copy-start | bytes 36868
  13.3 21.5 %copy-start.10 = (f32[3072]{0:T(1024)S(1)}, f32[3072]{0:T(1024)}, u32[]{:S(2)}) copy-start(f32[3072]{0:T(1024)} %param.17) | copy-start | bytes 36868
  14.2 79.7 %collective-permute-start = (bf16[40,1024]{0,1:T(8,128)(2,1)}, bf16[40,1024]{0,1:T(8,128)(2,1)}, u32[]{:S(2)}, u32[]{:S(2)}) collective-permute-start(bf16[40,1024]{0,1:T(8,128)(2,1)} %get-tuple-element.18), channel_id=1, source_target_pairs={{0,1},{1,2},{2,3},{3,4},{4,5},{5,6},{6,7},{7,8},{8,9},{9,10},{10,1... | collective-permute-start | bytes 245768 | tf_op jit(solution)/shard_map/ppermute | solution.py:28
  19.7 75.2 %collective-permute-start.1 = (bf16[40,1024]{0,1:T(8,128)(2,1)}, bf16[40,1024]{0,1:T(8,128)(2,1)S(1)}, u32[]{:S(2)}, u32[]{:S(2)}) collective-permute-start(bf16[40,1024]{0,1:T(8,128)(2,1)} %get-tuple-element.19), channel_id=1, source_target_pairs={{1,0},{2,1},{3,2},{4,3},{5,4},{6,5},{7,6},{8,7},{9,8},{10,9},{11,1... | collective-permute-start | bytes 245768 | tf_op jit(solution)/shard_map/ppermute | solution.py:30
  34.8 5.3 copy-start.11
  34.8 5.3 copy-start.12
  38.6 76.2 %collective-permute-start.2 = (bf16[40,3072]{1,0:T(8,128)(2,1)}, bf16[40,3072]{1,0:T(8,128)(2,1)}, u32[]{:S(2)}, u32[]{:S(2)}) collective-permute-start(bf16[40,3072]{1,0:T(8,128)(2,1)} %copy.34), channel_id=1, source_target_pairs={{0,16},{16,0},{1,17},{17,1},{2,18},{18,2},{3,19},{19,3},{4,20},{20... | collective-permute-start | bytes 737288 | tf_op jit(solution)/shard_map/ppermute | solution.py:17
  40.1 1.6 slice-start.8
  90.0 5.1 copy-start.7
  95.7 8.2 %slice-start = ((s8[6291456]{0:T(1024)(128)(4,1)}), s8[4194304]{0:T(1024)(128)(4,1)S(1)}, s32[]{:S(2)}) async-start(s8[6291456]{0:T(1024)(128)(4,1)} %bitcast.259), calls=%async_computation.1 | async-start | bytes 8388608
  99.0 4.9 slice-start.1
  182.1 6.0 %copy-start.1 = (f32[1,40,8192]{1,2,0:T(8,128)S(1)}, f32[1,40,8192]{1,2,0:T(8,128)}, u32[]{:S(2)}) copy-start(f32[1,40,8192]{1,2,0:T(8,128)} %copy.38) | copy-start | bytes 3932164
  188.2 3.2 copy-start
  196.4 33.7 %collective-permute-start.3 = (bf16[80,1024]{0,1:T(8,128)(2,1)}, bf16[80,1024]{0,1:T(8,128)(2,1)S(1)}, u32[]{:S(2)}, u32[]{:S(2)}) collective-permute-start(bf16[80,1024]{0,1:T(8,128)(2,1)} %get-tuple-element.16), channel_id=1, source_target_pairs={{0,1},{1,2},{2,3},{3,4},{4,5},{5,6},{6,7},{7,8},{8,9},{9,10},{10,1... | collective-permute-start | bytes 491528 | tf_op jit(solution)/shard_map/ppermute | solution.py:28
  200.6 29.5 %collective-permute-start.4 = (bf16[80,1024]{0,1:T(8,128)(2,1)}, bf16[80,1024]{0,1:T(8,128)(2,1)S(1)}, u32[]{:S(2)}, u32[]{:S(2)}) collective-permute-start(bf16[80,1024]{0,1:T(8,128)(2,1)} %get-tuple-element.17), channel_id=1, source_target_pairs={{1,0},{2,1},{3,2},{4,3},{5,4},{6,5},{7,6},{8,7},{9,8},{10,9},{11,1... | collective-permute-start | bytes 491528 | tf_op jit(solution)/shard_map/ppermute | solution.py:30
  219.3 122.5 %collective-permute-start.5 = (bf16[80,3072]{1,0:T(8,128)(2,1)}, bf16[80,3072]{1,0:T(8,128)(2,1)}, u32[]{:S(2)}, u32[]{:S(2)}) collective-permute-start(bf16[80,3072]{1,0:T(8,128)(2,1)} %copy.42), channel_id=1, source_target_pairs={{0,16},{16,0},{1,17},{17,1},{2,18},{18,2},{3,19},{19,3},{4,20},{20... | collective-permute-start | bytes 1474568 | tf_op jit(solution)/shard_map/ppermute | solution.py:17
  242.0 10.2 %slice-start.2 = ((s8[6291456]{0:T(1024)(128)(4,1)}), s8[2097152]{0:T(1024)(128)(4,1)S(1)}, s32[]{:S(2)}) async-start(s8[6291456]{0:T(1024)(128)(4,1)} %bitcast.261), calls=%async_computation.3 | async-start | bytes 4194304
  245.2 7.0 %slice-start.3 = ((s8[6291456]{0:T(1024)(128)(4,1)}), s8[4194304]{0:T(1024)(128)(4,1)S(1)}, s32[]{:S(2)}) async-start(s8[6291456]{0:T(1024)(128)(4,1)} %bitcast.261), calls=%async_computation.4 | async-start | bytes 8388608
  260.0 7.4 %copy-start.4 = (bf16[80,16,512]{2,1,0:T(8,128)(2,1)}, bf16[80,16,512]{2,1,0:T(8,128)(2,1)S(1)}, u32[]{:S(2)}) copy-start(bf16[80,16,512]{2,1,0:T(8,128)(2,1)S(1)} %copy.56) | copy-start | bytes 3932164
  263.8 13.7 %slice-start.4 = ((s8[6291456]{0:T(1024)(128)(4,1)}), s8[2097152]{0:T(1024)(128)(4,1)S(1)}, s32[]{:S(2)}) async-start(s8[6291456]{0:T(1024)(128)(4,1)} %bitcast.263), calls=%async_computation.5 | async-start | bytes 4194304
  270.5 7.0 %slice-start.5 = ((s8[6291456]{0:T(1024)(128)(4,1)}), s8[4194304]{0:T(1024)(128)(4,1)S(1)}, s32[]{:S(2)}) async-start(s8[6291456]{0:T(1024)(128)(4,1)} %bitcast.263), calls=%async_computation.6 | async-start | bytes 8388608
  274.0 3.5 copy-start.5
  287.7 1.1 copy-start.2
  292.1 16.3 %slice-start.6 = ((s8[6291456]{0:T(1024)(128)(4,1)}), s8[2097152]{0:T(1024)(128)(4,1)S(1)}, s32[]{:S(2)}) async-start(s8[6291456]{0:T(1024)(128)(4,1)} %bitcast.265), calls=%async_computation.7 | async-start | bytes 4194304
  300.5 8.0 %slice-start.7 = ((s8[6291456]{0:T(1024)(128)(4,1)}), s8[4194304]{0:T(1024)(128)(4,1)S(1)}, s32[]{:S(2)}) async-start(s8[6291456]{0:T(1024)(128)(4,1)} %bitcast.265), calls=%async_computation.8 | async-start | bytes 8388608
  304.5 4.0 copy-start.3
  308.4 2.3 copy-start.6
  526.0 7.9 %copy-start.8 = (f32[120,120]{1,0:T(8,128)S(1)}, f32[120,120]{1,0:T(8,128)}, u32[]{:S(2)}) copy-start(f32[120,120]{1,0:T(8,128)} %get-tuple-element.6) | copy-start | bytes 172804
Sparse Core Ops, SparseCore 0:
  376.3 125.1 all-reduce.5
where the time goes:
time: 547 us; the launch traced here: 543 us
  matrix products  126 us (23%)
  waiting for transfers between devices  125 us (23%)
  local copies, waits for them, and re-layouts  122 us (22%)
  other arithmetic  98.6 us (18%)
  blocking collectives  41.7 us (8%)
  between operations  15.8 us (3%)
  starting transfers between devices  12.4 us (2%)
    psum x1, waiting for transfers between devices, shards(): lax.psum((jnp.dot(search, search.T, precision=highest), jnp.dot(search, i...  125 us
    dot_general x40, matrix products, typed_product(): lax.dot_general(flattened, table_set[type_id], (((1,), (contract,)), ((),...  93 us
    unnamed x53, local copies, waits for them, and re-layouts  67.2 us
    psum x1, blocking collectives, shards(): lax.psum((jnp.sum(vec_modes * vec_modes, axis=1), jnp.sum(vec_modes * ima...  41.7 us
    scatter-add x2, other arithmetic, operate(): return images.at[:, rows].add(received)  39.2 us
    gather x2, local copies, waits for them, and re-layouts, operate(): values = jnp.take(vectors, rows, axis=1) * weights[None, :]  26.6 us
    dot_general x1, matrix products, shards(): jnp.dot(search, image_all.T, precision=highest)  13.1 us
    another operation x3, other arithmetic, shards(): chol = jnp.linalg.cholesky(gram_b)  11.6 us
  transfers between devices with their start and end apart: 7, of which 1 were waited for; matrix products, arithmetic and copies ran while one was open for 42% of the time, Pallas kernels for 0%

commit v1 on v0

--- a/solution.py
+++ b/solution.py
@@ -7,6 +7,11 @@
 NTYPE = 4
 NBR = 16
 IFACE = 3072
+
+
+def by_each_axis(value, first, second):
+    inner = lax.psum(value, first)
+    return lax.psum(inner, second)
 
 
 def for_sending(shard):
@@ -116,12 +121,13 @@
     search = jnp.concatenate([vec_modes, pair], axis=0)
     image_all = jnp.concatenate([image_x, image_wp], axis=0)
     ndof = 2.0 * lax.axis_size("dom") * NBR * BS
-    summed_b, summed_a = lax.psum(
+    summed_b, summed_a = by_each_axis(
         (
             jnp.dot(search, search.T, precision=highest),
             jnp.dot(search, image_all.T, precision=highest),
         ),
-        ("field", "dom"),
+        "dom",
+        "field",
     )
     gram_b = summed_b / ndof
     gram_a = (summed_a + summed_a.T) / (2.0 * ndof)

time: 547 us -> 549 us (level)
    psum x1 -> x2, waiting for transfers between devices: 125 us -> 126 us  [the longest x1 107 us: by_each_axis(): inner = lax.psum(value, first)]
  transfers between devices with their start and end apart: 7 -> 8, of which waited for: 1 -> 2; matrix products, arithmetic and copies ran while one was open for 42% -> 42% of each run, Pallas kernels for 0% -> 0%
where the time goes in v1:
time: 549 us; the launch traced here: 544 us
  matrix products  126 us (23%)
  waiting for transfers between devices  126 us (23%)
  local copies, waits for them, and re-layouts  122 us (22%)
  other arithmetic  98.4 us (18%)
  blocking collectives  41.7 us (8%)
  between operations  15.9 us (3%)
  starting transfers between devices  12.7 us (2%)
    psum x1, waiting for transfers between devices, by_each_axis(): inner = lax.psum(value, first)  107 us
    dot_general x40, matrix products, typed_product(): lax.dot_general(flattened, table_set[type_id], (((1,), (contract,)), ((),...  93 us
    unnamed x53, local copies, waits for them, and re-layouts  67.2 us
    psum x1, blocking collectives, shards(): lax.psum((jnp.sum(vec_modes * vec_modes, axis=1), jnp.sum(vec_modes * ima...  41.7 us
    scatter-add x2, other arithmetic, operate(): return images.at[:, rows].add(received)  39.2 us
    gather x2, local copies, waits for them, and re-layouts, operate(): values = jnp.take(vectors, rows, axis=1) * weights[None, :]  26.6 us
    psum x1, waiting for transfers between devices, by_each_axis(): return lax.psum(inner, second)  19.4 us
    dot_general x1, matrix products, shards(): jnp.dot(search, image_all.T, precision=highest)  13.1 us
  transfers between devices with their start and end apart: 8, of which 2 were waited for; matrix products, arithmetic and copies ran while one was open for 42% of the time, Pallas kernels for 0%

profile of v1, /device:TPU:0, one launch (start us, length us, event | category | flops | bytes accessed | tf_op | source)
XLA Modules:
  0.0 543.7 jit_solution(9636974827668413956)
XLA Ops:
  7.2 3.7 copy.30
  10.9 2.4 bitcast_convert_fusion
  14.2 5.6 %collective-permute-start = (bf16[40,1024]{0,1:T(8,128)(2,1)}, bf16[40,1024]{0,1:T(8,128)(2,1)}, u32[]{:S(2)}, u32[]{:S(2)}) collective-permute-start(bf16[40,1024]{0,1:T(8,128)(2,1)} %get-tuple-element.20), channel_id=1, source_target_pairs={{0,1},{1,2},{2,3},{3,4},{4,5},{5,6},{6,7},{7,8},{8,9},{9,10},{10,1... | collective-permute-start | bytes 245768 | tf_op jit(solution)/shard_map/ppermute | solution.py:33
  19.8 1.3 collective-permute-start.1
  21.7 13.1 %gather_fusion = f32[3072,40]{1,0:T(8,128)} fusion(f32[40,8192]{0,1:T(8,128)} %bitcast.254, s32[3072]{0:T(1024)S(1)} %broadcast_clamp_fusion), kind=kCustom, calls=%fused_computation | custom fusion | bytes 995328 | tf_op jit(solution)/shard_map/jit(_take)/gather | solution.py:84
  34.9 2.8 fusion.24
  38.7 1.5 copy.32
  40.7 1.1 slice-done.8
  41.8 41.6 %copy.52 = bf16[1,1,4,512,512]{2,4,3,1,0:T(8,128)(2,1)} copy(bf16[1,1,4,512,512]{4,3,2,1,0:T(8,128)(2,1)S(1)} %slice-done.8) | data formatting | bytes 4194304
  83.3 6.4 %gather_fusion.1 = bf16[512,4]{1,0:T(8,128)(2,1)S(1)} fusion(bf16[4,512,512]{0,2,1:T(8,128)(2,1)} %bitcast.58, s32[512]{0:T(512)S(1)} %bitcast.269), kind=kCustom, calls=%fused_computation.1 | custom fusion | bytes 12288 | tf_op jit(solution)/shard_map/jit(diagonal)/gather | solution.py:111
  90.0 3.9 copy.38
  95.7 1.7 convolution_multiply_fusion.19
  97.5 1.6 convolution_multiply_fusion.15
  99.1 1.7 convolution_multiply_fusion.11
  100.8 1.6 convolution_multiply_fusion.7
  102.4 1.5 convolution_multiply_fusion.3
  112.1 2.7 copy.47
  116.3 19.6 %scatter_fusion = f32[40,8192]{0,1:T(8,128)} fusion(f32[40,8192]{0,1:T(8,128)} %bitcast.256, s32[3072]{0:T(1024)S(1)} %bitcast.271, f32[3072,40]{1,0:T(8,128)S(1)} %copy.36), kind=kCustom, calls=%fused_computation.3 | custom fusion | flops 122880 | bytes 1486848 | tf_op jit(solution)/shard_map/scatter-add | solution.py:86
  135.9 4.6 multiply_reduce_fusion
  140.4 41.7 %all-reduce.2 = (f32[40]{0:T(128)S(1)}, f32[40]{0:T(128)S(1)}) all-reduce(f32[40]{0:T(128)S(1)} %get-tuple-element.4, f32[40]{0:T(128)S(1)} %get-tuple-element.3), channel_id=1, replica_groups=mesh['field'=2,'dom'=16] {'field','dom'}, use_global_device_ids=true, to_apply=%region_2.3 | all-reduce | flops 80 | bytes 640 | tf_op jit(solution)/shard_map/psum | solution.py:106
  182.1 6.0 %subtract_divide_fusion = f32[40,8192]{0,1:T(8,128)S(1)} fusion(f32[40,8192]{0,1:T(8,128)} %scatter_fusion, f32[8192]{0:T(1024)S(1)} %bitcast.273, f32[40]{0:T(128)S(1)} %div.33, f32[1,40,8192]{1,2,0:T(8,128)} %copy.30), kind=kLoop, calls=%fused_computation.12 | loop fusion | flops 983040 | bytes 3965088 | tf_op jit(solution)/shard_map/div | solution.py:117
  188.2 3.2 fusion.174
  191.3 4.2 pad_maximum_fusion
  196.4 4.2 collective-permute-start.3
  200.6 1.3 collective-permute-start.4
  201.9 13.5 %gather_fusion.2 = f32[3072,80]{1,0:T(8,128)} fusion(f32[80,8192]{0,1:T(8,128)} %get-tuple-element.12, s32[3072]{0:T(1024)S(1)} %broadcast_clamp_fusion), kind=kCustom, calls=%fused_computation.2 | custom fusion | bytes 1978368 | tf_op jit(solution)/shard_map/jit(_take)/gather | solution.py:84
  215.5 2.8 fusion.25
  219.3 10.8 %fusion.178 = f32[120,120]{0,1:T(8,128)} fusion(f32[120,8192]{0,1:T(8,128)} %pad_maximum_fusion), kind=kOutput, calls=%fused_computation.259 | convolution fusion | flops 1415577600 | bytes 3989760 | tf_op jit(solution)/shard_map/dot_general | solution.py:126
  230.1 7.7 %pad_maximum_fusion.2 = bf16[80,10240]{0,1:T(8,128)(2,1)S(1)} fusion(bf16[80,1024]{0,1:T(8,128)(2,1)S(1)} %collective-permute-done.4, bf16[80,8192]{0,1:T(8,128)(2,1)S(1)} %get-tuple-element.11, bf16[80,1024]{0,1:T(8,128)(2,1)S(1)} %collective-permute-done.3), kind=kLoop, calls=%fused_computation.15 | loop fusion | flops 4915200 | bytes 3276800 | tf_op jit(solution)/shard_map/concatenate | solution.py:31
  237.8 4.2 fusion.175
  242.0 3.2 copy.53
  245.3 3.6 fusion.26
  248.8 3.4 fusion.29
  252.2 2.4 fusion.32
  254.6 2.3 fusion.35
  256.9 3.1 copy.56
  260.0 3.8 fusion.39
  263.8 3.6 fusion.45
  267.4 3.1 copy.57
  270.5 3.5 fusion.43
  274.0 3.5 fusion.49
  277.5 2.4 fusion.51
  279.8 2.4 fusion.55
  282.2 2.4 fusion.57
  284.6 3.1 copy.55
  288.8 3.4 fusion.61
  292.1 3.9 fusion.67
  296.0 4.4 copy.54
  300.4 4.0 fusion.63
  304.4 4.0 fusion.69
  308.4 2.3 fusion.73
  310.7 2.4 fusion.75
  313.1 2.3 fusion.79
  315.5 2.4 fusion.81
  317.8 19.0 %add_add_fusion = f32[80,16,512]{2,1,0:T(8,128)} fusion(f32[80,16,512]{2,1,0:T(8,128)} %fusion.43, f32[80,16,512]{2,1,0:T(8,128)} %fusion.49, f32[80,16,512]{2,1,0:T(8,128)} %fusion.55, f32[80,16,512]{2,1,0:T(8,128)} %fusion.39, f32[80,16,512]{2,1,0:T(8,128)} %fusion.45, f32[80,16,512]{2,1,0:T(8,128)} %fusion.51, f32[80,16,512]{2,1,0:T(8,128)} %fusion.57, ...), kind=kOutput, calls=%fused_computation.16 | convolution fusion | flops 696647680 | bytes 54265088 | tf_op jit(solution)/shard_map/dot_general | solution.py:49
  336.8 4.9 copy.49
  341.8 1.1 convert_bitcast_fusion
  343.4 19.6 %scatter_fusion.1 = f32[80,8192]{0,1:T(8,128)} fusion(f32[80,8192]{0,1:T(8,128)} %bitcast.258, s32[3072]{0:T(1024)S(1)} %bitcast.272, f32[3072,80]{1,0:T(8,128)S(1)} %copy.44), kind=kCustom, calls=%fused_computation.4 | custom fusion | flops 245760 | bytes 2961408 | tf_op jit(solution)/shard_map/scatter-add | solution.py:86
  363.0 13.1 %fusion = f32[120,120]{1,0:T(8,128)} fusion(f32[120,8192]{0,1:T(8,128)} %pad_maximum_fusion, f32[80,8192]{0,1:T(8,128)} %scatter_fusion.1, f32[40,8192]{0,1:T(8,128)} %scatter_fusion), kind=kOutput, calls=%fused_computation.8 | convolution fusion | flops 1416560640 | bytes 7921920 | tf_op jit(solution)/shard_map/dot_general | solution.py:127
  376.5 107.0 %all-reduce.8.cloned.1.call-done = (f32[120,120]{0,1:T(8,128)}, f32[120,120]{1,0:T(8,128)}) async-done(((f32[120,120]{0,1:T(8,128)}, f32[120,120]{1,0:T(8,128)}), (f32[120,120]{0,1:T(8,128)}, f32[120,120]{1,0:T(8,128)})) %all-reduce.8.cloned.1.call-update) | async-done | bytes 115216 | tf_op jit(solution)/shard_map/psum | solution.py:13
  483.6 19.4 %all-reduce.10.cloned.1.call-done = (f32[120,120]{0,1:T(8,128)}, f32[120,120]{1,0:T(8,128)}) async-done(((f32[120,120]{0,1:T(8,128)}, f32[120,120]{1,0:T(8,128)}), (f32[120,120]{0,1:T(8,128)}, f32[120,120]{1,0:T(8,128)})) %all-reduce.10.cloned.1.call-update) | async-done | bytes 115216 | tf_op jit(solution)/shard_map/psum | solution.py:14
  504.7 11.0 %cholesky.16 = f32[120,120]{1,0:T(8,128)S(1)} custom-call(f32[120,120]{1,0:T(8,128)S(1)} %fusion.152), custom_call_target="Cholesky" | custom-call | tf_op jit(solution)/shard_map/jit(cholesky)/cholesky | solution.py:134
  517.1 9.2 %custom-call.10 = f32[1,120,120]{1,2,0:T(8,128)S(1)} custom-call(f32[1,120,120]{2,1,0:T(8,128)S(1)} %fusion.145), custom_call_target="InvertDiagBlocksLowerTriangular" | custom-call | tf_op jit(solution)/shard_map/jit(_solve_triangular)/triangular_solve | solution.py:137
  527.2 7.9 %convolution_bitcast_fusion = f32[1,120,8192]{2,1,0:T(8,128)} fusion(f32[120,8192]{0,1:T(8,128)} %pad_maximum_fusion, f32[1,120,120]{1,2,0:T(8,128)S(1)} %custom-call.10), kind=kOutput, calls=%fused_computation.5 | convolution fusion | flops 1415577600 | bytes 7921920 | tf_op jit(solution)/shard_map/jit(_solve_triangular)/triangular_solve | solution.py:137
  (110 shorter events, 23.0 us)
Async XLA Ops:
  7.2 476.4 %all-reduce.8.cloned.1.call-start = ((), (), s32[]{:S(2)}) async-start(), calls=%async_computation | async-start | bytes 245760 | tf_op jit(solution)/shard_map/psum | solution.py:13
  10.9 10.1 %copy-start.9 = (s32[1,3072]{1,0:T(1,128)S(1)}, s32[1,3072]{1,0:T(1,128)}, u32[]{:S(2)}) copy-start(s32[1,3072]{1,0:T(1,128)} %param.15) | copy-start | bytes 36868
  13.3 21.5 %copy-start.10 = (f32[3072]{0:T(1024)S(1)}, f32[3072]{0:T(1024)}, u32[]{:S(2)}) copy-start(f32[3072]{0:T(1024)} %param.17) | copy-start | bytes 36868
  14.2 79.7 %collective-permute-start = (bf16[40,1024]{0,1:T(8,128)(2,1)}, bf16[40,1024]{0,1:T(8,128)(2,1)}, u32[]{:S(2)}, u32[]{:S(2)}) collective-permute-start(bf16[40,1024]{0,1:T(8,128)(2,1)} %get-tuple-element.20), channel_id=1, source_target_pairs={{0,1},{1,2},{2,3},{3,4},{4,5},{5,6},{6,7},{7,8},{8,9},{9,10},{10,1... | collective-permute-start | bytes 245768 | tf_op jit(solution)/shard_map/ppermute | solution.py:33
  19.8 75.2 %collective-permute-start.1 = (bf16[40,1024]{0,1:T(8,128)(2,1)}, bf16[40,1024]{0,1:T(8,128)(2,1)S(1)}, u32[]{:S(2)}, u32[]{:S(2)}) collective-permute-start(bf16[40,1024]{0,1:T(8,128)(2,1)} %get-tuple-element.21), channel_id=1, source_target_pairs={{1,0},{2,1},{3,2},{4,3},{5,4},{6,5},{7,6},{8,7},{9,8},{10,9},{11,1... | collective-permute-start | bytes 245768 | tf_op jit(solution)/shard_map/ppermute | solution.py:35
  34.9 5.3 copy-start.11
  34.9 5.3 copy-start.12
  38.7 76.2 %collective-permute-start.2 = (bf16[40,3072]{1,0:T(8,128)(2,1)}, bf16[40,3072]{1,0:T(8,128)(2,1)}, u32[]{:S(2)}, u32[]{:S(2)}) collective-permute-start(bf16[40,3072]{1,0:T(8,128)(2,1)} %copy.34), channel_id=1, source_target_pairs={{0,16},{16,0},{1,17},{17,1},{2,18},{18,2},{3,19},{19,3},{4,20},{20... | collective-permute-start | bytes 737288 | tf_op jit(solution)/shard_map/ppermute | solution.py:22
  40.2 1.6 slice-start.8
  90.0 5.2 copy-start.7
  95.7 8.2 %slice-start = ((s8[6291456]{0:T(1024)(128)(4,1)}), s8[4194304]{0:T(1024)(128)(4,1)S(1)}, s32[]{:S(2)}) async-start(s8[6291456]{0:T(1024)(128)(4,1)} %bitcast.259), calls=%async_computation.2 | async-start | bytes 8388608
  99.1 4.9 slice-start.1
  182.1 6.0 %copy-start.1 = (f32[1,40,8192]{1,2,0:T(8,128)S(1)}, f32[1,40,8192]{1,2,0:T(8,128)}, u32[]{:S(2)}) copy-start(f32[1,40,8192]{1,2,0:T(8,128)} %copy.38) | copy-start | bytes 3932164
  188.2 3.2 copy-start
  196.4 33.7 %collective-permute-start.3 = (bf16[80,1024]{0,1:T(8,128)(2,1)}, bf16[80,1024]{0,1:T(8,128)(2,1)S(1)}, u32[]{:S(2)}, u32[]{:S(2)}) collective-permute-start(bf16[80,1024]{0,1:T(8,128)(2,1)} %get-tuple-element.18), channel_id=1, source_target_pairs={{0,1},{1,2},{2,3},{3,4},{4,5},{5,6},{6,7},{7,8},{8,9},{9,10},{10,1... | collective-permute-start | bytes 491528 | tf_op jit(solution)/shard_map/ppermute | solution.py:33
  200.6 29.5 %collective-permute-start.4 = (bf16[80,1024]{0,1:T(8,128)(2,1)}, bf16[80,1024]{0,1:T(8,128)(2,1)S(1)}, u32[]{:S(2)}, u32[]{:S(2)}) collective-permute-start(bf16[80,1024]{0,1:T(8,128)(2,1)} %get-tuple-element.19), channel_id=1, source_target_pairs={{1,0},{2,1},{3,2},{4,3},{5,4},{6,5},{7,6},{8,7},{9,8},{10,9},{11,1... | collective-permute-start | bytes 491528 | tf_op jit(solution)/shard_map/ppermute | solution.py:35
  219.3 122.5 %collective-permute-start.5 = (bf16[80,3072]{1,0:T(8,128)(2,1)}, bf16[80,3072]{1,0:T(8,128)(2,1)}, u32[]{:S(2)}, u32[]{:S(2)}) collective-permute-start(bf16[80,3072]{1,0:T(8,128)(2,1)} %copy.42), channel_id=1, source_target_pairs={{0,16},{16,0},{1,17},{17,1},{2,18},{18,2},{3,19},{19,3},{4,20},{20... | collective-permute-start | bytes 1474568 | tf_op jit(solution)/shard_map/ppermute | solution.py:22
  242.0 10.2 %slice-start.2 = ((s8[6291456]{0:T(1024)(128)(4,1)}), s8[2097152]{0:T(1024)(128)(4,1)S(1)}, s32[]{:S(2)}) async-start(s8[6291456]{0:T(1024)(128)(4,1)} %bitcast.261), calls=%async_computation.4 | async-start | bytes 4194304
  245.2 7.0 %slice-start.3 = ((s8[6291456]{0:T(1024)(128)(4,1)}), s8[4194304]{0:T(1024)(128)(4,1)S(1)}, s32[]{:S(2)}) async-start(s8[6291456]{0:T(1024)(128)(4,1)} %bitcast.261), calls=%async_computation.5 | async-start | bytes 8388608
  260.0 7.4 %copy-start.4 = (bf16[80,16,512]{2,1,0:T(8,128)(2,1)}, bf16[80,16,512]{2,1,0:T(8,128)(2,1)S(1)}, u32[]{:S(2)}) copy-start(bf16[80,16,512]{2,1,0:T(8,128)(2,1)S(1)} %copy.56) | copy-start | bytes 3932164
  263.8 13.7 %slice-start.4 = ((s8[6291456]{0:T(1024)(128)(4,1)}), s8[2097152]{0:T(1024)(128)(4,1)S(1)}, s32[]{:S(2)}) async-start(s8[6291456]{0:T(1024)(128)(4,1)} %bitcast.263), calls=%async_computation.6 | async-start | bytes 4194304
  270.5 7.0 %slice-start.5 = ((s8[6291456]{0:T(1024)(128)(4,1)}), s8[4194304]{0:T(1024)(128)(4,1)S(1)}, s32[]{:S(2)}) async-start(s8[6291456]{0:T(1024)(128)(4,1)} %bitcast.263), calls=%async_computation.7 | async-start | bytes 8388608
  274.0 3.5 copy-start.5
  287.7 1.1 copy-start.2
  292.1 16.3 %slice-start.6 = ((s8[6291456]{0:T(1024)(128)(4,1)}), s8[2097152]{0:T(1024)(128)(4,1)S(1)}, s32[]{:S(2)}) async-start(s8[6291456]{0:T(1024)(128)(4,1)} %bitcast.265), calls=%async_computation.8 | async-start | bytes 4194304
  300.4 8.0 %slice-start.7 = ((s8[6291456]{0:T(1024)(128)(4,1)}), s8[4194304]{0:T(1024)(128)(4,1)S(1)}, s32[]{:S(2)}) async-start(s8[6291456]{0:T(1024)(128)(4,1)} %bitcast.265), calls=%async_computation.9 | async-start | bytes 8388608
  304.4 4.0 copy-start.3
  308.4 2.3 copy-start.6
  376.2 126.8 %all-reduce.10.cloned.1.call-start = ((), (), s32[]{:S(2)}) async-start(), calls=%async_computation.1 | async-start | bytes 245760 | tf_op jit(solution)/shard_map/psum | solution.py:14
  527.2 7.9 %copy-start.8 = (f32[120,120]{1,0:T(8,128)S(1)}, f32[120,120]{1,0:T(8,128)}, u32[]{:S(2)}) copy-start(f32[120,120]{1,0:T(8,128)} %get-tuple-element.10) | copy-start | bytes 172804
Sparse Core Ops, SparseCore 0:
  376.3 107.1 all-reduce.7
  485.9 16.9 all-reduce.9
